TPU v7x, 32 devices: a whole 2x2x4 slice. The times are simulated.
32 devices in a mesh: gx: 2 (over y), gy: 4 (over x, core), gz: 4 (over z).
Axes of the slice: x: 2, y: 2, z: 4, core: 2. Of those that a mesh axis runs over, the one named last changes fastest.
Arguments:
- targets: float32 [512, 512, 512], P('gx', 'gy', 'gz'), may hold values from -6 to 6
- basis_first: float32 [512, 512], replicated, may hold values from -0.25 to 0.25
- basis_second: float32 [512, 512], replicated, may hold values from -0.25 to 0.25
- basis_third: float32 [512, 512], replicated, may hold values from -0.25 to 0.25
- eigen_first: float32 [512], replicated, may hold values from 0.1 to 1
- eigen_second: float32 [512], replicated, may hold values from 0.1 to 1
- eigen_third: float32 [512], replicated, may hold values from 0.1 to 1
- noise: float32 [1], replicated, may hold values from 0.5 to 1
Outputs:
- weights: float32 [512, 512, 512], P('gx', 'gy', 'gz')
All inputs are finite; a program needn't handle non-finite values.
Results may differ from a plain program's by a relative error of at most 0.000071.
Values sent between devices are 32-bit elements; how exact they have to be, the bound alone decides.
A program may use at most 128 MiB of HBM per device.

v0:
```python
import jax
import jax.numpy as jnp
from jax import lax
from jax.experimental import pallas as pl
from jax.experimental.pallas import tpu as pltpu
from jax.sharding import PartitionSpec as P

MESH = pl.DeviceIdType.MESH
CHUNKS = 4
HIGH = lax.Precision.HIGH


def offsets_of(sizes, names):
    found = [{}]
    for name in names:
        found = [{**base, name: step} for base in found for step in range(sizes[name])]
    found = [one for one in found if any(one.values())]
    far = lambda one: min(one.get("gz", 0), sizes["gz"] - one.get("gz", 0))
    return sorted(found, key=lambda one: -far(one))


def kernel(sizes, tasks, n_in, fresh, *refs):
    ins, outs, sems = refs[:n_in], refs[n_in:-1 - 2 * len(tasks)], refs[-1 - 2 * len(tasks):]
    me = {name: lax.axis_index(name) for name in sizes}
    everyone = "gz" if any("gz" in task[1] for task in tasks) else ""
    reach = ("gz", "gx", "gy") if everyone else ("gx", "gy")
    shift = lambda off: {n: (lax.rem(me[n] + s, sizes[n]) if s else me[n]) for n, s in off.items()}

    barrier = pltpu.get_barrier_semaphore()
    greeted = offsets_of(sizes, reach)
    for off in greeted:
        pl.semaphore_signal(barrier, inc=1, device_id=shift(off), device_id_type=MESH)
    pl.semaphore_wait(barrier, len(greeted))

    def rank(where, names):
        total = 0
        for n in names:
            total = total * sizes[n] + where[n]
        return total

    def parts(task, source, target, where_from, where_to):
        gathers, names, first, depth = task[0], task[1], task[4], task[5]
        grid, spine = (target, source) if gathers else (source, target)
        holder = where_from if gathers else where_to
        other = where_to if gathers else where_from
        rows, cols = spine.shape[1], spine.shape[2]
        run = spine.shape[0] // max(1, _count(sizes, names))
        k_at = rank(other, names) * run + first
        spine_part = spine.at[pl.ds(k_at, depth)]
        row_at = pl.multiple_of(rank(holder, names[:-1]) * rows, 8)
        col_at = pl.multiple_of(rank(holder, names[-1:]) * cols, 128)
        grid_part = grid.at[:, pl.ds(row_at, rows), pl.ds(col_at, cols)]
        return (spine_part, grid_part) if gathers else (grid_part, spine_part)

    running = []
    for t, task in enumerate(tasks):
        source = ins[task[2]]
        target = outs[task[3]]
        send, recv = sems[2 * t], sems[2 * t + 1]
        for s, off in enumerate(offsets_of(sizes, task[1])):
            peer = shift(off)
            src, dst = parts(task, source, target, me, peer)
            copy = pltpu.make_async_remote_copy(
                src_ref=src, dst_ref=dst, send_sem=send.at[s], recv_sem=recv.at[s],
                device_id=peer, device_id_type=MESH,
            )
            copy.start()
            running.append(copy)
        src, dst = parts(task, source, target, me, me)
        own = pltpu.make_async_copy(src, dst, sems[-1].at[t])
        own.start()
        running.append(own)
    for copy in running:
        copy.wait()


def _count(sizes, names):
    total = 1
    for n in names:
        total *= sizes[n]
    return total


def exchange(sizes, cid, tasks, sources, shapes, carried=None):
    carried = carried or {}
    n_src = len(sources)
    aliases = {n_src + i: out for i, out in enumerate(sorted(carried))}
    extra = [carried[out] for out in sorted(carried)]
    scratch = []
    for task in tasks:
        n = _count(sizes, task[1]) - 1
        scratch += [pltpu.SemaphoreType.DMA((n,)), pltpu.SemaphoreType.DMA((n,))]
    scratch.append(pltpu.SemaphoreType.DMA((len(tasks),)))
    any_space = pl.BlockSpec(memory_space=pl.ANY)

    def body(*refs):
        kernel(sizes, tasks, n_src + len(extra), None, *refs)

    return pl.pallas_call(
        body,
        out_shape=[jax.ShapeDtypeStruct(s, jnp.float32) for s in shapes],
        in_specs=[any_space] * (n_src + len(extra)),
        out_specs=[any_space] * len(shapes),
        scratch_shapes=scratch,
        input_output_aliases=aliases,
        compiler_params=pltpu.CompilerParams(collective_id=cid, has_side_effects=True),
        name=f"exchange_{cid}",
    )(*sources, *extra)


def solution(mesh):
    sizes = {name: mesh.shape[name] for name in ("gx", "gy", "gz")}
    near, every = ("gx", "gy"), ("gz", "gx", "gy")

    def per_device(targets, b1, b2, b3, e1, e2, e3, noise):
        rows, cols, deep = targets.shape
        n1, n2, n3 = b1.shape[0], b2.shape[0], b3.shape[0]
        run = deep // _count(sizes, near)
        chunks = min(CHUNKS, run)
        part = run // chunks
        na, nb = n1 // _count(sizes, ("gz", "gx")), n2 // sizes["gy"]
        slab, whole, spine = (part, n1, n2), (n3, na, nb), (deep, rows, cols)
        lead = jnp.transpose(targets, (2, 0, 1))

        def forward(x):
            x = jnp.einsum("kij,jb->kib", x, b2, precision=HIGH)
            return jnp.einsum("ia,kib->kab", b1, x, precision=HIGH)

        def backward(x):
            x = jnp.einsum("kab,jb->kaj", x, b2, precision=HIGH)
            return jnp.einsum("ia,kaj->kij", b1, x, precision=HIGH)

        (x,) = exchange(sizes, 0, [(True, near, 0, 0, 0, part)], [lead], [slab])
        gathered = None
        for q in range(chunks):
            v = forward(x)
            tasks, sources, shapes = [(False, every, 0, 0, q * part, part)], [v], [whole]
            if q + 1 < chunks:
                tasks.append((True, near, 1, 1, (q + 1) * part, part))
                sources.append(lead)
                shapes.append(slab)
            got = exchange(sizes, 1 + q, tasks, sources, shapes, {} if gathered is None else {0: gathered})
            gathered = got[0]
            x = got[1] if q + 1 < chunks else None

        here = {n: lax.axis_index(n) for n in sizes}
        l1 = lax.dynamic_slice_in_dim(e1, (here["gz"] * sizes["gx"] + here["gx"]) * na, na, 0)
        l2 = lax.dynamic_slice_in_dim(e2, here["gy"] * nb, nb, 0)
        rotated = jnp.einsum("kab,kc->acb", gathered, b3, precision=HIGH)
        spectrum = l1[:, None, None] * l2[None, None, :] * e3[None, :, None] + noise[0]
        scaled = rotated / spectrum
        u = jnp.einsum("acb,kc->kab", scaled, b3, precision=HIGH)

        base = 1 + chunks
        (w,) = exchange(sizes, base, [(True, every, 0, 0, 0, part)], [u], [slab])
        result = None
        for q in range(chunks):
            y = backward(w)
            tasks, sources, shapes = [(False, near, 0, 0, q * part, part)], [y], [spine]
            if q + 1 < chunks:
                tasks.insert(0, (True, every, 1, 1, (q + 1) * part, part))
                sources.append(u)
                shapes.append(slab)
            got = exchange(sizes, base + 1 + q, tasks, sources, shapes, {} if result is None else {0: result})
            result = got[0]
            w = got[1] if q + 1 < chunks else None
        return jnp.transpose(result, (1, 2, 0))

    return jax.shard_map(
        per_device,
        mesh=mesh,
        in_specs=(P("gx", "gy", "gz"), P(), P(), P(), P(), P(), P(), P()),
        out_specs=P("gx", "gy", "gz"),
        check_vma=False,
    )
```

profile of v0, /device:TPU:0, one launch (start us, length us, event | category | flops | bytes accessed | tf_op | source)
XLA Modules:
  0.0 1134.5 jit_solution(11930887173730119821)
XLA Ops:
  0.0 0.0 copy-start
  0.0 17.5 %copy.15 = f32[256,128,128]{1,0,2:T(8,128)} copy(f32[256,128,128]{2,1,0:T(8,128)} %param.8) | data formatting | bytes 33554432 | tf_op args[0]
  17.5 0.0 copy-start.2
  17.5 49.8 %exchange_0.1 = f32[4,512,512]{2,1,0:T(8,128)} custom-call(f32[128,256,128]{2,1,0:T(8,128)} %bitcast.83), custom_call_target="tpu_custom_call" | custom-call | tf_op jit(solution)/shard_map/exchange_0/pallas_call | solution.py:99
  67.4 0.0 copy-done.2
  67.4 0.0 copy-start.3
  67.4 6.2 fusion.32
  73.6 0.0 copy-done.3
  73.6 5.2 convolution_bitcast_fusion.7.refs_0_
  78.8 101.8 %exchange_1.1 = (f32[512,64,128]{2,1,0:T(8,128)}, f32[4,512,512]{2,1,0:T(8,128)}) custom-call(f32[4,512,512]{2,1,0:T(8,128)} %convolution_bitcast_fusion.7.refs_0_, f32[128,256,128]{2,1,0:T(8,128)} %bitcast.84), custom_call_target="tpu_custom_call" | custom-call | tf_op jit(solution)/shard_map/exchange_1/pallas_call | solution.py:99
  180.6 6.1 fusion.30
  186.7 5.2 convolution_bitcast_fusion.6.refs_0_
  191.8 109.0 %exchange_2.1 = (f32[512,64,128]{2,1,0:T(8,128)}, f32[4,512,512]{2,1,0:T(8,128)}) custom-call(f32[4,512,512]{2,1,0:T(8,128)} %convolution_bitcast_fusion.6.refs_0_, f32[128,256,128]{2,1,0:T(8,128)} %bitcast.85, f32[512,64,128]{2,1,0:T(8,128)} %get-tuple-element.18.refs_2_), custom_call_target="tpu_custom_call", output_to_operand_aliasing={{0}: (2, {})} | custom-call | tf_op jit(solution)/shard_map/exchange_2/pallas_call | solution.py:99
  300.9 6.3 fusion.28
  307.2 5.2 convolution_bitcast_fusion.5.refs_0_
  312.4 108.4 %exchange_3.1 = (f32[512,64,128]{2,1,0:T(8,128)}, f32[4,512,512]{2,1,0:T(8,128)}) custom-call(f32[4,512,512]{2,1,0:T(8,128)} %convolution_bitcast_fusion.5.refs_0_, f32[128,256,128]{2,1,0:T(8,128)} %bitcast.86, f32[512,64,128]{2,1,0:T(8,128)} %get-tuple-element.20.refs_2_), custom_call_target="tpu_custom_call", output_to_operand_aliasing={{0}: (2, {})} | custom-call | tf_op jit(solution)/shard_map/exchange_3/pallas_call | solution.py:99
  420.8 5.3 fusion.26
  426.1 5.2 convolution_bitcast_fusion.4.refs_0_
  431.3 83.7 %exchange_4.1 = f32[512,64,128]{2,1,0:T(8,128)} custom-call(f32[4,512,512]{2,1,0:T(8,128)} %convolution_bitcast_fusion.4.refs_0_, f32[512,64,128]{2,1,0:T(8,128)} %get-tuple-element.22.refs_1_), custom_call_target="tpu_custom_call", output_to_operand_aliasing={{}: (1, {})} | custom-call | tf_op jit(solution)/shard_map/exchange_4/pallas_call | solution.py:99
  515.0 0.0 copy-done
  515.1 0.0 copy-start.4
  515.1 34.1 %fusion.1 = f32[64,128,512]{2,1,0:T(8,128)} fusion(f32[512,64,128]{2,1,0:T(8,128)} %exchange_4.1, f32[512,512]{1,0:T(8,128)S(1)} %copy-done), kind=kOutput, calls=%fused_computation.2 | convolution fusion | flops 12884901888 | bytes 34603008 | tf_op jit(solution)/shard_map/kab,kc->acb/dot_general | solution.py:149
  549.2 0.8 dynamic_slice.6
  549.9 0.8 dynamic_slice.7
  550.7 0.1 broadcast_multiply_fusion
  551.4 0.0 copy-done.4
  551.4 20.6 %fusion = f32[64,128,512]{2,1,0:T(8,128)} fusion(f32[64,128,512]{2,1,0:T(8,128)} %fusion.1, f32[]{:T(128)} %bitcast.78, f32[512]{0:T(512)S(1)} %copy-done.4, f32[64,128]{1,0:T(8,128)S(1)} %broadcast_multiply_fusion, f32[512,512]{1,0:T(8,128)S(1)} %copy-done), kind=kOutput, calls=%fused_computation.1 | convolution fusion | flops 12897484800 | bytes 34637828 | tf_op jit(solution)/shard_map/acb,kc->kab/dot_general | solution.py:152
  572.1 16.5 %copy.19 = f32[64,128,512]{1,0,2:T(8,128)} copy(f32[64,128,512]{2,1,0:T(8,128)} %fusion) | data formatting | bytes 33554432 | tf_op jit(solution)/shard_map/acb,kc->kab/dot_general | solution.py:152
  588.6 95.0 %exchange_5.1 = f32[4,512,512]{2,1,0:T(8,128)} custom-call(f32[512,64,128]{2,1,0:T(8,128)} %bitcast.79), custom_call_target="tpu_custom_call" | custom-call | tf_op jit(solution)/shard_map/exchange_5/pallas_call | solution.py:99
  683.6 6.5 fusion.24
  690.1 5.3 convolution_bitcast_fusion.3.refs_0_
  695.4 120.1 %exchange_6.1 = (f32[128,256,128]{2,1,0:T(8,128)}, f32[4,512,512]{2,1,0:T(8,128)}) custom-call(f32[4,512,512]{2,1,0:T(8,128)} %convolution_bitcast_fusion.3.refs_0_, f32[512,64,128]{2,1,0:T(8,128)} %bitcast.80), custom_call_target="tpu_custom_call" | custom-call | tf_op jit(solution)/shard_map/exchange_6/pallas_call | solution.py:99
  815.5 6.5 fusion.22
  822.1 5.1 convolution_bitcast_fusion.2.refs_0_
  827.2 108.3 %exchange_7.1 = (f32[128,256,128]{2,1,0:T(8,128)}, f32[4,512,512]{2,1,0:T(8,128)}) custom-call(f32[4,512,512]{2,1,0:T(8,128)} %convolution_bitcast_fusion.2.refs_0_, f32[512,64,128]{2,1,0:T(8,128)} %bitcast.81, f32[128,256,128]{2,1,0:T(8,128)} %get-tuple-element.24.refs_2_), custom_call_target="tpu_custom_call", output_to_operand_aliasing={{0}: (2, {})} | custom-call | tf_op jit(solution)/shard_map/exchange_7/pallas_call | solution.py:99
  935.5 6.5 fusion.20
  942.1 5.3 convolution_bitcast_fusion.1.refs_0_
  947.4 108.7 %exchange_8.1 = (f32[128,256,128]{2,1,0:T(8,128)}, f32[4,512,512]{2,1,0:T(8,128)}) custom-call(f32[4,512,512]{2,1,0:T(8,128)} %convolution_bitcast_fusion.1.refs_0_, f32[512,64,128]{2,1,0:T(8,128)} %bitcast.82, f32[128,256,128]{2,1,0:T(8,128)} %get-tuple-element.26.refs_2_), custom_call_target="tpu_custom_call", output_to_operand_aliasing={{0}: (2, {})} | custom-call | tf_op jit(solution)/shard_map/exchange_8/pallas_call | solution.py:99
  1056.1 6.5 fusion.18
  1062.7 5.0 convolution_bitcast_fusion.refs_0_
  1067.7 48.7 %exchange_9.1 = f32[128,256,128]{2,1,0:T(8,128)} custom-call(f32[4,512,512]{2,1,0:T(8,128)} %convolution_bitcast_fusion.refs_0_, f32[128,256,128]{2,1,0:T(8,128)} %get-tuple-element.28.refs_1_), custom_call_target="tpu_custom_call", output_to_operand_aliasing={{}: (1, {})} | custom-call | tf_op jit(solution)/shard_map/exchange_9/pallas_call | solution.py:99
  1116.4 0.0 copy-start.1
  1116.4 17.7 %copy.24 = f32[256,128,128]{2,1,0:T(8,128)} copy(f32[256,128,128]{1,0,2:T(8,128)} %bitcast.87) | data formatting | bytes 33554432 | tf_op jit(solution)/shard_map/transpose | solution.py:167
  1134.1 0.0 copy-done.1
Async XLA Ops:
  0.0 515.0 %copy-start = (f32[512,512]{1,0:T(8,128)S(1)}, f32[512,512]{1,0:T(8,128)}, u32[]{:S(2)}) copy-start(f32[512,512]{1,0:T(8,128)} %param.11) | copy-start | bytes 3145732
  17.5 49.8 %copy-start.2 = (f32[512,512]{1,0:T(8,128)S(1)}, f32[512,512]{1,0:T(8,128)}, u32[]{:S(2)}) copy-start(f32[512,512]{1,0:T(8,128)} %param.10) | copy-start | bytes 3145732
  67.4 6.2 copy-start.3
  515.1 36.4 %copy-start.4 = (f32[512]{0:T(512)S(1)}, f32[512]{0:T(512)}, u32[]{:S(2)}) copy-start(f32[512]{0:T(512)} %param.14) | copy-start | bytes 6148
  1116.4 17.7 %copy-start.1 = (f32[512,512]{1,0:T(8,128)S(1)}, f32[512,512]{1,0:T(8,128)}, u32[]{:S(2)}) copy-start(f32[512,512]{1,0:T(8,128)} %param.11) | copy-start | bytes 3145732
where the time goes:
time: 1150 us; the launch traced here: 1130 us
  Pallas kernels  934 us (81%)
  matrix products  146 us (13%)
  local copies, waits for them, and re-layouts  53.2 us (5%)
    pallas_call x10, Pallas kernels, exchange(): pl.pallas_call(body, out_shape=[jax.ShapeDtypeStruct(s, jnp.float32) for...  934 us
    dot_general x1, matrix products, per_device(): rotated = jnp.einsum('kab,kc->acb', gathered, b3, precision=HIGH)  34.1 us
    dot_general x4, matrix products, backward(): x = jnp.einsum('kab,jb->kaj', x, b2, precision=HIGH)  26.1 us
    dot_general x4, matrix products, forward(): x = jnp.einsum('kij,jb->kib', x, b2, precision=HIGH)  24 us

commit v1 on v0

v1 whole, which is shorter than its diff:
```python
import jax
import jax.numpy as jnp
from jax import lax
from jax.experimental import pallas as pl
from jax.experimental.pallas import tpu as pltpu
from jax.sharding import PartitionSpec as P

MESH = pl.DeviceIdType.MESH
AHEAD = 3
SLOTS = 8
EARLY = 2
GRAIN = 8


def split(x):
    high = x.astype(jnp.bfloat16)
    low = (x - high.astype(jnp.float32)).astype(jnp.bfloat16)
    return high, low


def dot3(left, right):
    one = lambda a, b: jnp.dot(a, b, preferred_element_type=jnp.float32)
    return one(left[0], right[0]) + (one(left[0], right[1]) + one(left[1], right[0]))


def offsets_of(sizes, names):
    found = [{}]
    for name in names:
        found = [{**base, name: step} for base in found for step in range(sizes[name])]
    found = [one for one in found if any(one.values())]
    far = lambda one: min(one.get("gz", 0), sizes["gz"] - one.get("gz", 0))
    return sorted(found, key=lambda one: -far(one))


def kernel(sizes, dims, lead, b1, b2, b3, e1, e2, e3, noise, out,
           slab, made, whole, w1, w1t, w2, w2t, w3, w3t,
           base_sem, near_send, near_recv, far_send, far_recv, back_send, back_recv, out_send, out_recv):
    run, rows, cols, na, nb, n3 = dims
    me = {name: lax.axis_index(name) for name in sizes}
    shift = lambda off: {n: (lax.rem(me[n] + s, sizes[n]) if s else me[n]) for n, s in off.items()}
    near_of = lambda w: w["gx"] * sizes["gy"] + w["gy"]
    full = lambda w: {**me, **w}
    near = offsets_of(sizes, ("gx", "gy"))
    every = offsets_of(sizes, ("gz", "gx", "gy"))
    slots = min(SLOTS, run)

    i_at = lambda w: (pl.ds(pl.multiple_of(w["gx"] * rows, 8), rows), pl.ds(pl.multiple_of(w["gy"] * cols, 128), cols))
    a_from = lambda w: (w["gz"] * sizes["gx"] + w["gx"]) * na
    a_at = lambda w: (pl.ds(pl.multiple_of(a_from(w), 8), na), pl.ds(pl.multiple_of(w["gy"] * nb, 128), nb))
    k_from = lambda w: (w["gz"] * len_near + near_of(w)) * run
    len_near = sizes["gx"] * sizes["gy"]

    loads = [pltpu.make_async_copy(b, made.at[q % slots], base_sem.at[q]) for q, b in enumerate((b1, b2, b3))]
    loads[0].start()
    loads[1].start()
    barrier = pltpu.get_barrier_semaphore()
    for off in every:
        pl.semaphore_signal(barrier, inc=1, device_id=full(shift(off)), device_id_type=MESH)
    pl.semaphore_wait(barrier, len(every))

    def send_near(p):
        for off in near:
            peer = full(shift(off))
            pltpu.make_async_remote_copy(
                src_ref=lead.at[near_of(peer) * run + p], dst_ref=slab.at[(p, *i_at(me))],
                send_sem=near_send, recv_sem=near_recv.at[p], device_id=peer, device_id_type=MESH).start()
        pltpu.make_async_copy(lead.at[near_of(me) * run + p], slab.at[(p, *i_at(me))], near_recv.at[p]).start()

    def send_far(p, slot):
        for off in every:
            peer = full(shift(off))
            pltpu.make_async_remote_copy(
                src_ref=made.at[(slot, *a_at(peer))], dst_ref=whole.at[k_from(me) + p],
                send_sem=far_send.at[slot], recv_sem=far_recv, device_id=peer, device_id_type=MESH).start()

    def send_back(p, first, depth):
        piece = (pl.ds(pl.multiple_of(a_from(me) + first, 8), depth), a_at(me)[1])
        for off in every:
            peer = full(shift(off))
            pltpu.make_async_remote_copy(
                src_ref=whole.at[k_from(peer) + p, pl.ds(first, depth)], dst_ref=slab.at[(p, *piece)],
                send_sem=back_send, recv_sem=back_recv.at[p], device_id=peer, device_id_type=MESH).start()

    def send_out(p, slot):
        for off in near:
            peer = full(shift(off))
            pltpu.make_async_remote_copy(
                src_ref=made.at[(slot, *i_at(peer))], dst_ref=out.at[near_of(me) * run + p],
                send_sem=out_send.at[slot], recv_sem=out_recv, device_id=peer, device_id_type=MESH).start()
        pltpu.make_async_copy(made.at[(slot, *i_at(me))], out.at[near_of(me) * run + p], out_send.at[slot]).start()

    def await_bytes(ref, sem):
        pltpu.make_async_copy(ref, ref, sem).wait()

    def keep(pair, x):
        pair[0], pair[1] = split(x)

    for p in range(min(AHEAD, run)):
        send_near(p)

    loads[0].wait()
    loads[1].wait()
    keep(w1, made[0])
    keep(w1t, made[0].T)
    keep(w2, made[1 % slots])
    keep(w2t, made[1 % slots].T)
    loads[2].start()
    loads[2].wait()
    keep(w3, made[2 % slots])
    keep(w3t, made[2 % slots].T)

    def forward(p, carry):
        slot = lax.rem(p, slots)
        await_bytes(slab.at[p], near_recv.at[p])

        @pl.when(p >= slots)
        def _():
            await_bytes(whole.at[pl.ds(0, len(every))], far_send.at[slot])

        x = dot3(split(slab[p]), (w2[0], w2[1]))
        made[slot] = dot3((w1t[0], w1t[1]), split(x))
        send_far(p, slot)
        whole[k_from(me) + p] = made[(slot, *a_at(me))]

        @pl.when(p + AHEAD < run)
        def _():
            send_near(p + AHEAD)

        return carry

    lax.fori_loop(0, run, forward, 0)
    await_bytes(whole.at[pl.ds(0, run * len(every))], far_recv)

    second = e2[pl.ds(me["gy"], 1), :]
    third = e3[...]

    def middle(q, carry):
        first = pl.multiple_of(q * GRAIN, GRAIN)
        scale = e1[pl.ds(pl.multiple_of(a_from(me) + first, 8), GRAIN), :] * second
        scale = scale.reshape(1, GRAIN * nb)
        x = whole[:, pl.ds(first, GRAIN), :].reshape(n3, GRAIN * nb)
        x = dot3((w3t[0], w3t[1]), split(x))
        x = x / (scale * third + noise[0])
        x = dot3((w3[0], w3[1]), split(x))
        whole[:, pl.ds(first, GRAIN), :] = x.reshape(n3, GRAIN, nb)
        for p in range(min(EARLY, run)):
            send_back(p, first, GRAIN)
        return carry

    lax.fori_loop(0, na // GRAIN, middle, 0)

    def rest(p, carry):
        send_back(p, 0, na)
        return carry

    lax.fori_loop(min(EARLY, run), run, rest, 0)

    for p in range(run - slots, run):
        await_bytes(whole.at[pl.ds(0, len(every))], far_send.at[p % slots])

    def backward(p, carry):
        slot = lax.rem(p, slots)
        await_bytes(whole.at[pl.ds(0, len(every))], back_recv.at[p])
        slab[(p, *a_at(me))] = whole[k_from(me) + p]

        @pl.when(p >= slots)
        def _():
            await_bytes(lead.at[pl.ds(0, len_near)], out_send.at[slot])

        x = dot3(split(slab[p]), (w2t[0], w2t[1]))
        made[slot] = dot3((w1[0], w1[1]), split(x))
        send_out(p, slot)
        return carry

    lax.fori_loop(0, run, backward, 0)
    for p in range(run - slots, run):
        await_bytes(lead.at[pl.ds(0, len_near)], out_send.at[p % slots])
    await_bytes(lead.at[pl.ds(0, run * len(near))], near_send)
    await_bytes(whole.at[pl.ds(0, run * len(every))], back_send)
    await_bytes(lead.at[pl.ds(0, run * len(near))], out_recv)


def solution(mesh):
    sizes = {name: mesh.shape[name] for name in ("gx", "gy", "gz")}

    def per_device(targets, b1, b2, b3, e1, e2, e3, noise):
        rows, cols, deep = targets.shape
        n1, n2, n3 = b1.shape[0], b2.shape[0], b3.shape[0]
        run = deep // (sizes["gx"] * sizes["gy"])
        na, nb = n1 // (sizes["gz"] * sizes["gx"]), n2 // sizes["gy"]
        slots = min(SLOTS, run)
        lead = jnp.transpose(targets, (2, 0, 1))
        space = pl.BlockSpec(memory_space=pl.ANY)
        held = pl.BlockSpec(memory_space=pltpu.VMEM)
        dma = pltpu.SemaphoreType.DMA

        def body(*refs):
            kernel(sizes, (run, rows, cols, na, nb, n3), *refs)

        pair = lambda n: pltpu.VMEM((2, n, n), jnp.bfloat16)
        result = pl.pallas_call(
            body,
            out_shape=jax.ShapeDtypeStruct((deep, rows, cols), jnp.float32),
            in_specs=[space] * 4 + [held] * 3 + [pl.BlockSpec(memory_space=pltpu.SMEM)],
            out_specs=space,
            scratch_shapes=[
                pltpu.VMEM((run, n1, n2), jnp.float32),
                pltpu.VMEM((slots, n1, n2), jnp.float32),
                pltpu.VMEM((n3, na, nb), jnp.float32),
                pair(n1), pair(n1), pair(n2), pair(n2), pair(n3), pair(n3),
                dma((3,)), dma, dma((run,)), dma((slots,)), dma, dma, dma((run,)), dma((slots,)), dma,
            ],
            compiler_params=pltpu.CompilerParams(
                collective_id=0, has_side_effects=True, vmem_limit_bytes=67043328),
            name="solve",
        )(lead, b1, b2, b3, jnp.broadcast_to(e1[:, None], (n1, nb)), e2.reshape(-1, nb), e3[:, None], noise)
        return jnp.transpose(result, (1, 2, 0))

    return jax.shard_map(
        per_device,
        mesh=mesh,
        in_specs=(P("gx", "gy", "gz"), P(), P(), P(), P(), P(), P(), P()),
        out_specs=P("gx", "gy", "gz"),
        check_vma=False,
    )
```

time: 1150 us -> 830 us (0.72)
  Pallas kernels: 934 us -> 781 us
  matrix products: 146 us -> 0 us
  local copies, waits for them, and re-layouts: 53.2 us -> 38.1 us
    pallas_call x10 -> x1, Pallas kernels: 934 us -> 781 us  [per_device(): pl.pallas_call(body, out_shape=jax.ShapeDtypeStruct((deep, rows, cols), j...]
    dot_general x18 -> x0, matrix products: 146 us -> none  [the longest x1 34.1 us: per_device(): rotated = jnp.einsum('kab,kc->acb', gathered, b3, precision=HIGH)]
    dot_general x1 -> x0, local copies, waits for them, and re-layouts: 16.5 us -> none  [per_device(): u = jnp.einsum('acb,kc->kab', scaled, b3, precision=HIGH)]
where the time goes in v1:
time: 830 us; the launch traced here: 820 us
  Pallas kernels  781 us (94%)
  local copies, waits for them, and re-layouts  38.1 us (5%)
    pallas_call x1, Pallas kernels, per_device(): pl.pallas_call(body, out_shape=jax.ShapeDtypeStruct((deep, rows, cols), j...  781 us
    transpose x1, local copies, waits for them, and re-layouts, per_device(): return jnp.transpose(result, (1, 2, 0))  17.6 us
    unnamed x1, local copies, waits for them, and re-layouts  17.4 us

profile of v1, /device:TPU:0, one launch (start us, length us, event | category | flops | bytes accessed | tf_op | source)
XLA Modules:
  0.0 819.9 jit_solution(17356187639664696639)
XLA Ops:
  0.7 1.5 broadcast_in_dim.4.refs_4_
  2.2 1.5 copy.12.refs_6_
  3.7 17.4 %copy.11 = f32[256,128,128]{1,0,2:T(8,128)} copy(f32[256,128,128]{2,1,0:T(8,128)} %param.8) | data formatting | bytes 33554432 | tf_op args[0]
  21.1 781.1 %solve.1 = f32[128,256,128]{2,1,0:T(8,128)} custom-call(f32[128,256,128]{2,1,0:T(8,128)} %bitcast.5, f32[512,512]{1,0:T(8,128)} %refs_1_.1, f32[512,512]{1,0:T(8,128)} %refs_2_.1, f32[512,512]{1,0:T(8,128)} %refs_3_.1, f32[512,128]{1,0:T(8,128)} %broadcast_in_dim.4.refs_4_, f32[4,128]{1,0:T(4,128)} %bitcast.7, f32[512,1]{1,0:T(8,128)} %copy.12.refs_6_, ...), custom_call_target="tpu_custom_call" | custom-call | tf_op jit(solution)/shard_map/solve/pallas_call | solution.py:201
  802.3 17.6 %copy.13 = f32[256,128,128]{2,1,0:T(8,128)} copy(f32[256,128,128]{1,0,2:T(8,128)} %bitcast.4) | data formatting | bytes 33554432 | tf_op jit(solution)/shard_map/transpose | solution.py:217

commit v2 on v1

--- a/solution.py
+++ b/solution.py
@@ -6,10 +6,14 @@
 from jax.sharding import PartitionSpec as P
 
 MESH = pl.DeviceIdType.MESH
-AHEAD = 3
+AHEAD = 5
 SLOTS = 8
 EARLY = 2
 GRAIN = 8
+STRIP = 16
+FIRST = 1
+DEPTH = 4
+TURN = 32
 
 
 def split(x):
@@ -29,12 +33,12 @@
         found = [{**base, name: step} for base in found for step in range(sizes[name])]
     found = [one for one in found if any(one.values())]
     far = lambda one: min(one.get("gz", 0), sizes["gz"] - one.get("gz", 0))
-    return sorted(found, key=lambda one: -far(one))
-
-
-def kernel(sizes, dims, lead, b1, b2, b3, e1, e2, e3, noise, out,
-           slab, made, whole, w1, w1t, w2, w2t, w3, w3t,
-           base_sem, near_send, near_recv, far_send, far_recv, back_send, back_recv, out_send, out_recv):
+    return sorted(found, key=lambda one: (-one.get("gx", 0) * sizes["gy"] - one.get("gy", 0), -far(one)))
+
+
+def kernel(sizes, dims, targets, b1, b2, b3, e1, e2, e3, noise, lead, out,
+           slab, made, whole, w1, w1t, w2, w2t, w3, w3t, taken, turned,
+           base_sem, take_sem, turn_sem, near_send, near_recv, far_send, far_recv, back_send, back_recv, out_send, out_recv):
     run, rows, cols, na, nb, n3 = dims
     me = {name: lax.axis_index(name) for name in sizes}
     shift = lambda off: {n: (lax.rem(me[n] + s, sizes[n]) if s else me[n]) for n, s in off.items()}
@@ -50,21 +54,32 @@
     k_from = lambda w: (w["gz"] * len_near + near_of(w)) * run
     len_near = sizes["gx"] * sizes["gy"]
 
-    loads = [pltpu.make_async_copy(b, made.at[q % slots], base_sem.at[q]) for q, b in enumerate((b1, b2, b3))]
-    loads[0].start()
-    loads[1].start()
+    deep, strip = lead.shape[0], min(STRIP, rows)
+    strips, depth = rows // strip, min(DEPTH, rows // strip)
+    held = [slots - 3 + q for q in range(3)]
+    loads = [pltpu.make_async_copy(b, made.at[held[q]], base_sem.at[q]) for q, b in enumerate((b1, b2, b3))]
+    take = lambda q: pltpu.make_async_copy(
+        targets.at[pl.ds(q * strip, strip)], taken.at[lax.rem(q, depth)], take_sem.at[lax.rem(q, depth)])
+    turn = lambda q: pltpu.make_async_copy(
+        turned.at[lax.rem(q, depth)], lead.at[:, pl.ds(pl.multiple_of(q * strip, 8), strip)], turn_sem.at[lax.rem(q, depth)])
+    for q in range(depth):
+        take(q).start()
+    for load in loads:
+        load.start()
     barrier = pltpu.get_barrier_semaphore()
     for off in every:
         pl.semaphore_signal(barrier, inc=1, device_id=full(shift(off)), device_id_type=MESH)
     pl.semaphore_wait(barrier, len(every))
 
-    def send_near(p):
+    def send_near(p, first, depth):
+        piece = (pl.ds(pl.multiple_of(me["gx"] * rows + first, 8), depth), i_at(me)[1])
+        part = pl.ds(pl.multiple_of(first, 8), depth)
         for off in near:
             peer = full(shift(off))
             pltpu.make_async_remote_copy(
-                src_ref=lead.at[near_of(peer) * run + p], dst_ref=slab.at[(p, *i_at(me))],
+                src_ref=lead.at[near_of(peer) * run + p, part], dst_ref=slab.at[(p, *piece)],
                 send_sem=near_send, recv_sem=near_recv.at[p], device_id=peer, device_id_type=MESH).start()
-        pltpu.make_async_copy(lead.at[near_of(me) * run + p], slab.at[(p, *i_at(me))], near_recv.at[p]).start()
+        pltpu.make_async_copy(lead.at[near_of(me) * run + p, part], slab.at[(p, *piece)], near_recv.at[p]).start()
 
     def send_far(p, slot):
         for off in every:
@@ -95,19 +110,37 @@
     def keep(pair, x):
         pair[0], pair[1] = split(x)
 
-    for p in range(min(AHEAD, run)):
-        send_near(p)
-
-    loads[0].wait()
-    loads[1].wait()
-    keep(w1, made[0])
-    keep(w1t, made[0].T)
-    keep(w2, made[1 % slots])
-    keep(w2t, made[1 % slots].T)
-    loads[2].start()
-    loads[2].wait()
-    keep(w3, made[2 % slots])
-    keep(w3t, made[2 % slots].T)
+    def settle(q):
+        turn(q).wait()
+        for p in range(FIRST):
+            send_near(p, q * strip, strip)
+
+    def turn_strip(q, carry):
+        slot = lax.rem(q, depth)
+        take(q).wait()
+
+        @pl.when(q >= depth)
+        def _():
+            settle(q - depth)
+
+        turned[slot] = taken[slot].reshape(strip * cols, deep).T.reshape(deep, strip, cols)
+        turn(q).start()
+
+        @pl.when(q + depth < strips)
+        def _():
+            take(q + depth).start()
+
+        return carry
+
+    lax.fori_loop(0, strips, turn_strip, 0)
+    for q in range(strips - depth, strips):
+        settle(q)
+    for p in range(FIRST, min(AHEAD, run)):
+        send_near(p, 0, rows)
+    for load in loads:
+        load.wait()
+    keep(w2, made[held[1]])
+    keep(w1t, made[held[0]].T)
 
     def forward(p, carry):
         slot = lax.rem(p, slots)
@@ -124,7 +157,14 @@
 
         @pl.when(p + AHEAD < run)
         def _():
-            send_near(p + AHEAD)
+            send_near(p + AHEAD, 0, rows)
+
+        @pl.when(p == 0)
+        def _():
+            keep(w1, made[held[0]])
+            keep(w2t, made[held[1]].T)
+            keep(w3, made[held[2]])
+            keep(w3t, made[held[2]].T)
 
         return carry
 
@@ -132,12 +172,11 @@
     await_bytes(whole.at[pl.ds(0, run * len(every))], far_recv)
 
     second = e2[pl.ds(me["gy"], 1), :]
-    third = e3[...]
+    third = jnp.broadcast_to(e3[...], (8, n3)).T[:, 0:1]
 
     def middle(q, carry):
         first = pl.multiple_of(q * GRAIN, GRAIN)
-        scale = e1[pl.ds(pl.multiple_of(a_from(me) + first, 8), GRAIN), :] * second
-        scale = scale.reshape(1, GRAIN * nb)
+        scale = jnp.concatenate([e1[a_from(me) + first + s] * second for s in range(GRAIN)], axis=1)
         x = whole[:, pl.ds(first, GRAIN), :].reshape(n3, GRAIN * nb)
         x = dot3((w3t[0], w3t[1]), split(x))
         x = x / (scale * third + noise[0])
@@ -180,6 +219,39 @@
     await_bytes(lead.at[pl.ds(0, run * len(near))], out_recv)
 
 
+def turn_back(x, y, taken, turned, take_sem, turn_sem):
+    depth, deep, strip, cols = taken.shape
+    strips = y.shape[0] // strip
+    part = lambda q: pl.ds(pl.multiple_of(q * strip, 8), strip)
+    take = lambda q: pltpu.make_async_copy(
+        x.at[:, part(q)], taken.at[lax.rem(q, depth)], take_sem.at[lax.rem(q, depth)])
+    turn = lambda q: pltpu.make_async_copy(
+        turned.at[lax.rem(q, depth)], y.at[part(q)], turn_sem.at[lax.rem(q, depth)])
+    for q in range(depth):
+        take(q).start()
+
+    def turn_strip(q, carry):
+        slot = lax.rem(q, depth)
+        take(q).wait()
+
+        @pl.when(q >= depth)
+        def _():
+            turn(q - depth).wait()
+
+        turned[slot] = taken[slot].reshape(deep, strip * cols).T.reshape(strip, cols, deep)
+        turn(q).start()
+
+        @pl.when(q + depth < strips)
+        def _():
+            take(q + depth).start()
+
+        return carry
+
+    lax.fori_loop(0, strips, turn_strip, 0)
+    for q in range(strips - depth, strips):
+        turn(q).wait()
+
+
 def solution(mesh):
     sizes = {name: mesh.shape[name] for name in ("gx", "gy", "gz")}
 
@@ -189,32 +261,49 @@
         run = deep // (sizes["gx"] * sizes["gy"])
         na, nb = n1 // (sizes["gz"] * sizes["gx"]), n2 // sizes["gy"]
         slots = min(SLOTS, run)
-        lead = jnp.transpose(targets, (2, 0, 1))
         space = pl.BlockSpec(memory_space=pl.ANY)
         held = pl.BlockSpec(memory_space=pltpu.VMEM)
+        small = pl.BlockSpec(memory_space=pltpu.SMEM)
+        strip, turn = min(STRIP, rows), min(TURN, rows)
+        depth, back = min(DEPTH, rows // strip), min(DEPTH, rows // turn)
+        spine = jax.ShapeDtypeStruct((deep, rows, cols), jnp.float32)
         dma = pltpu.SemaphoreType.DMA
 
         def body(*refs):
             kernel(sizes, (run, rows, cols, na, nb, n3), *refs)
 
         pair = lambda n: pltpu.VMEM((2, n, n), jnp.bfloat16)
-        result = pl.pallas_call(
+        _, result = pl.pallas_call(
             body,
-            out_shape=jax.ShapeDtypeStruct((deep, rows, cols), jnp.float32),
-            in_specs=[space] * 4 + [held] * 3 + [pl.BlockSpec(memory_space=pltpu.SMEM)],
-            out_specs=space,
+            out_shape=[spine, spine],
+            in_specs=[space] * 4 + [small] + [held] * 2 + [small],
+            out_specs=[space, space],
             scratch_shapes=[
                 pltpu.VMEM((run, n1, n2), jnp.float32),
                 pltpu.VMEM((slots, n1, n2), jnp.float32),
                 pltpu.VMEM((n3, na, nb), jnp.float32),
                 pair(n1), pair(n1), pair(n2), pair(n2), pair(n3), pair(n3),
-                dma((3,)), dma, dma((run,)), dma((slots,)), dma, dma, dma((run,)), dma((slots,)), dma,
+                pltpu.VMEM((depth, strip, cols, deep), jnp.float32),
+                pltpu.VMEM((depth, deep, strip, cols), jnp.float32),
+                dma((3,)), dma((depth,)), dma((depth,)), dma, dma((run,)), dma((slots,)), dma, dma, dma((run,)), dma((slots,)), dma,
             ],
             compiler_params=pltpu.CompilerParams(
                 collective_id=0, has_side_effects=True, vmem_limit_bytes=67043328),
             name="solve",
-        )(lead, b1, b2, b3, jnp.broadcast_to(e1[:, None], (n1, nb)), e2.reshape(-1, nb), e3[:, None], noise)
-        return jnp.transpose(result, (1, 2, 0))
+        )(targets, b1, b2, b3, e1, e2.reshape(-1, nb), e3.reshape(1, n3), noise)
+        return pl.pallas_call(
+            turn_back,
+            out_shape=jax.ShapeDtypeStruct((rows, cols, deep), jnp.float32),
+            in_specs=[space],
+            out_specs=space,
+            scratch_shapes=[
+                pltpu.VMEM((back, deep, turn, cols), jnp.float32),
+                pltpu.VMEM((back, turn, cols, deep), jnp.float32),
+                dma((back,)), dma((back,)),
+            ],
+            compiler_params=pltpu.CompilerParams(vmem_limit_bytes=67043328),
+            name="turn_back",
+        )(result)
 
     return jax.shard_map(
         per_device,

time: 830 us -> 801 us (0.965); the launches traced: 820 us -> 801 us
  local copies, waits for them, and re-layouts: 38.1 us -> 0 us
  Pallas kernels: 781 us -> 800 us
    pallas_call x1 -> x2, Pallas kernels: 781 us -> 800 us  [the longest x1 788 us: per_device(): pl.pallas_call(body, out_shape=[spine, spine], in_specs=[space] * 4 + [sm...]
    transpose x1 -> x0, local copies, waits for them, and re-layouts: 17.6 us -> none  [per_device(): return jnp.transpose(result, (1, 2, 0))]
    unnamed x1 -> x0, local copies, waits for them, and re-layouts: 17.4 us -> none
where the time goes in v2:
time: 801 us
  Pallas kernels  800 us (100%)
    pallas_call x1, Pallas kernels, per_device(): pl.pallas_call(body, out_shape=[spine, spine], in_specs=[space] * 4 + [sm...  788 us

profile of v2, /device:TPU:0, one launch (start us, length us, event | category | flops | bytes accessed | tf_op | source)
XLA Modules:
  0.0 801.0 jit_solution(14517916731774365255)
XLA Ops:
  0.7 788.3 %solve.1 = (f32[128,256,128]{2,1,0:T(8,128)}, f32[128,256,128]{2,1,0:T(8,128)}) custom-call(f32[256,128,128]{2,1,0:T(8,128)} %refs_0_.1, f32[512,512]{1,0:T(8,128)} %refs_1_.1, f32[512,512]{1,0:T(8,128)} %refs_2_.1, f32[512,512]{1,0:T(8,128)} %refs_3_.1, f32[512]{0:T(512)} %refs_4_.1, f32[4,128]{1,0:T(4,128)} %bitcast.2, f32[1,512]{1,0:T(1,128)} %bitcast.3, ...), custom_call_target="tpu_custom_call" | custom-call | tf_op jit(solution)/shard_map/solve/pallas_call | solution.py:276
  789.0 12.0 %turn_back.1 = f32[256,128,128]{2,1,0:T(8,128)} custom-call(f32[128,256,128]{2,1,0:T(8,128)} %get-tuple-element.6.x), custom_call_target="tpu_custom_call" | custom-call | tf_op jit(solution)/shard_map/turn_back/pallas_call | solution.py:294

commit v3 on v2

--- a/solution.py
+++ b/solution.py
@@ -13,6 +13,7 @@
 STRIP = 16
 FIRST = 1
 DEPTH = 4
+LAG = 2
 TURN = 32
 
 
@@ -32,8 +33,13 @@
     for name in names:
         found = [{**base, name: step} for base in found for step in range(sizes[name])]
     found = [one for one in found if any(one.values())]
-    far = lambda one: min(one.get("gz", 0), sizes["gz"] - one.get("gz", 0))
-    return sorted(found, key=lambda one: (-one.get("gx", 0) * sizes["gy"] - one.get("gy", 0), -far(one)))
+    core = lambda one: one.get("gy", 0) % 2
+    side = lambda one: one.get("gy", 0) // 2
+    hops = lambda one: (one.get("gx", 0) > 0) + (side(one) > 0)
+    deep = lambda one: one.get("gz", 0)
+    return sorted(found, key=lambda one: (
+        -core(one), -hops(one), one.get("gx", 0), side(one),
+        deep(one) < sizes["gz"] // 2, deep(one) == 0, deep(one)))
 
 
 def kernel(sizes, dims, targets, b1, b2, b3, e1, e2, e3, noise, lead, out,
@@ -41,7 +47,8 @@
            base_sem, take_sem, turn_sem, near_send, near_recv, far_send, far_recv, back_send, back_recv, out_send, out_recv):
     run, rows, cols, na, nb, n3 = dims
     me = {name: lax.axis_index(name) for name in sizes}
-    shift = lambda off: {n: (lax.rem(me[n] + s, sizes[n]) if s else me[n]) for n, s in off.items()}
+    paired = lambda n, s: me[n] ^ s if sizes[n] & (sizes[n] - 1) == 0 else lax.rem(me[n] + s, sizes[n])
+    shift = lambda off: {n: (paired(n, s) if s else me[n]) for n, s in off.items()}
     near_of = lambda w: w["gx"] * sizes["gy"] + w["gy"]
     full = lambda w: {**me, **w}
     near = offsets_of(sizes, ("gx", "gy"))
@@ -56,6 +63,7 @@
 
     deep, strip = lead.shape[0], min(STRIP, rows)
     strips, depth = rows // strip, min(DEPTH, rows // strip)
+    lag = min(LAG, depth)
     held = [slots - 3 + q for q in range(3)]
     loads = [pltpu.make_async_copy(b, made.at[held[q]], base_sem.at[q]) for q, b in enumerate((b1, b2, b3))]
     take = lambda q: pltpu.make_async_copy(
@@ -119,9 +127,9 @@
         slot = lax.rem(q, depth)
         take(q).wait()
 
-        @pl.when(q >= depth)
-        def _():
-            settle(q - depth)
+        @pl.when(q >= lag)
+        def _():
+            settle(q - lag)
 
         turned[slot] = taken[slot].reshape(strip * cols, deep).T.reshape(deep, strip, cols)
         turn(q).start()
@@ -133,7 +141,7 @@
         return carry
 
     lax.fori_loop(0, strips, turn_strip, 0)
-    for q in range(strips - depth, strips):
+    for q in range(strips - lag, strips):
         settle(q)
     for p in range(FIRST, min(AHEAD, run)):
         send_near(p, 0, rows)

time: 801 us -> 798 us (level)
  no operation moved by 1% of the time
where the time goes in v3:
time: 798 us
  Pallas kernels  798 us (100%)
    pallas_call x1, Pallas kernels, per_device(): pl.pallas_call(body, out_shape=[spine, spine], in_specs=[space] * 4 + [sm...  786 us

profile of v3, /device:TPU:0, one launch (start us, length us, event | category | flops | bytes accessed | tf_op | source)
XLA Modules:
  0.0 798.2 jit_solution(7719434184352342935)
XLA Ops:
  0.7 785.6 %solve.1 = (f32[128,256,128]{2,1,0:T(8,128)}, f32[128,256,128]{2,1,0:T(8,128)}) custom-call(f32[256,128,128]{2,1,0:T(8,128)} %refs_0_.1, f32[512,512]{1,0:T(8,128)} %refs_1_.1, f32[512,512]{1,0:T(8,128)} %refs_2_.1, f32[512,512]{1,0:T(8,128)} %refs_3_.1, f32[512]{0:T(512)} %refs_4_.1, f32[4,128]{1,0:T(4,128)} %bitcast.2, f32[1,512]{1,0:T(1,128)} %bitcast.3, ...), custom_call_target="tpu_custom_call" | custom-call | tf_op jit(solution)/shard_map/solve/pallas_call | solution.py:284
  786.2 12.0 %turn_back.1 = f32[256,128,128]{2,1,0:T(8,128)} custom-call(f32[128,256,128]{2,1,0:T(8,128)} %get-tuple-element.6.x), custom_call_target="tpu_custom_call" | custom-call | tf_op jit(solution)/shard_map/turn_back/pallas_call | solution.py:302
